TPU v7x, 32 devices: a whole 2x2x4 slice. The times are simulated.
32 devices in a mesh: ch: 4 (over z), sx: 4 (over x, core), sy: 2 (over y).
Axes of the slice: x: 2, y: 2, z: 4, core: 2. Of those that a mesh axis runs over, the one named last changes fastest.
Arguments:
- inputs: bfloat16 [768, 16, 4, 64], P('ch', 'sx', 'sy'), may hold values from -6 to 6
- pre_act: bfloat16 [768, 16, 4, 64], P('ch', 'sx', 'sy'), may hold values from -6 to 6
- out_grad: bfloat16 [768, 16, 4, 64], P('ch', 'sx', 'sy'), may hold values from -6 to 6
- weight_one: bfloat16 [27, 768, 768], P(None, 'ch'), may hold values from -0.0390625 to 0.0390625
- weight_two: bfloat16 [27, 768, 768], P(None, 'ch'), may hold values from -0.0390625 to 0.0390625
Outputs:
- input_grad: bfloat16 [768, 16, 4, 64], P('ch', 'sx', 'sy')
- filter_one_grad: float32 [27, 768, 768], P(None, 'ch')
- filter_two_grad: float32 [27, 768, 768], P(None, 'ch')
All inputs are finite; a program needn't handle non-finite values.
Results may differ from a plain program's by a relative error of at most 0.0049.
Values may be sent and summed in bfloat16 or wider, within the bound.
A program may use at most 192 MiB of HBM per device.

v0:
```python
import math
import jax
import jax.numpy as jnp
from jax import lax
from jax.sharding import PartitionSpec as P


def padded_2(cells, sides, width):
    for axis, dim in sides:
        count = lax.axis_size(axis)
        ends = count - 1
        head = lax.slice_in_dim(cells, 0, width, axis=dim)
        tail = lax.slice_in_dim(cells, cells.shape[dim] - width, cells.shape[dim], axis=dim)
        cells = jnp.concatenate(
            [
                lax.ppermute(tail, axis, [(i, (i + 1) % count) for i in range(ends)]),
                cells,
                lax.ppermute(head, axis, [((i + 1) % count, i) for i in range(ends)]),
            ],
            axis=dim,
        )
    return cells


def window(padded, offset, mirror):
    first = offset // 9
    second = offset // 3 % 3
    third = offset % 3
    if mirror:
        first, second, third = (2 - first, 2 - second, 2 - third)
    size_x = padded.shape[1] - 2
    size_y = padded.shape[2] - 2
    size_z = padded.shape[3] - 2
    part = padded[:, first : first + size_x, second : second + size_y, third : third + size_z]
    return part.reshape(padded.shape[0], size_x * size_y * size_z)


def pad_depth(array):
    return jnp.pad(array, ((0, 0), (0, 0), (0, 0), (1, 1)))


def contract_positions(left, right):
    return lax.dot_general(
        left, right, (((1,), (1,)), ((), ())), preferred_element_type=jnp.float32
    )


def contract_first(left, right):
    return lax.dot_general(
        left, right, (((0,), (0,)), ((), ())), preferred_element_type=jnp.float32
    )


def shards(inputs, pre_act, out_grad, weight_one, weight_two):
    shape = pre_act.shape
    positions = shape[1] * shape[2] * shape[3]
    full_in, full_grad = (
        lax.all_gather(inputs, "ch", axis=0, tiled=True),
        lax.all_gather(out_grad, "ch", axis=0, tiled=True),
    )
    inputs_pad = pad_depth(padded_2(full_in, (("sx", 1), ("sy", 2)), 1))
    grad_pad = pad_depth(padded_2(full_grad, (("sx", 1), ("sy", 2)), 1))
    active = jnp.maximum(pre_act, jnp.zeros((), pre_act.dtype))
    active_pad = pad_depth(padded_2(active, (("sx", 1), ("sy", 2)), 1))
    grad_flat = full_grad.reshape(full_grad.shape[0], positions)
    act_grad = jnp.zeros((shape[0], positions), jnp.float32)
    filter_two = []
    for offset in range(27):
        act_grad = act_grad + jnp.dot(
            weight_two[offset], window(grad_pad, offset, True), preferred_element_type=jnp.float32
        )
        filter_two.append(contract_positions(window(active_pad, offset, False), grad_flat))
    filter_two = jnp.stack(filter_two)
    delta = jnp.where(pre_act.reshape(shape[0], positions) > 0, act_grad, 0.0).astype(jnp.bfloat16)
    filter_one = []
    for offset in range(27):
        filter_one.append(contract_positions(delta, window(inputs_pad, offset, False)))
    filter_one = jnp.stack(filter_one)
    delta_rim = padded_2(delta.reshape(shape), (("sx", 1), ("sy", 2)), 1)
    delta_pad = pad_depth(delta_rim)
    partial_terms = jnp.zeros((weight_one.shape[2], positions), jnp.float32)
    for offset in range(27):
        partial_terms = partial_terms + contract_first(
            weight_one[offset], window(delta_pad, offset, True)
        )
    partial_terms = partial_terms.reshape(weight_one.shape[2], shape[1], shape[2], shape[3])
    input_grad = lax.psum_scatter(partial_terms, "ch", scatter_dimension=0, tiled=True).astype(
        jnp.bfloat16
    )
    filter_one, filter_two = lax.psum((filter_one, filter_two), ("sx", "sy"))
    factor = 1.0 / math.sqrt(positions * lax.axis_size("sx") * lax.axis_size("sy"))
    return (input_grad, filter_one * factor, filter_two * factor)


def solution(mesh):
    in_specs = (
        P("ch", "sx", "sy", None),
        P("ch", "sx", "sy", None),
        P("ch", "sx", "sy", None),
        P(None, "ch", None),
        P(None, "ch", None),
    )
    out_specs = (P("ch", "sx", "sy", None), P(None, "ch", None), P(None, "ch", None))
    return jax.shard_map(shards, mesh=mesh, in_specs=in_specs, out_specs=out_specs, check_vma=False)
```

profile of v0, /device:TPU:0, one launch (start us, length us, event | category | flops | bytes accessed | tf_op | source)
XLA Modules:
  0.0 700.8 jit_solution(13136925775982585537)
XLA Ops:
  9.7 3.0 collective-permute-start.12
  15.2 30.6 %all_gather.6 = bf16[768,4,2,64]{3,1,2,0:T(4,128)(2,1)S(1)} all-gather(bf16[192,4,2,64]{3,1,2,0:T(4,128)(2,1)S(1)} %copy.42), channel_id=1, replica_groups=mesh['ch'=4,'sx'=4,'sy'=2] {'ch'}, dimensions={0}, use_global_device_ids=true | all-gather | bytes 983040 | tf_op jit(solution)/shard_map/all_gather | solution.py:59
  47.6 3.7 collective-permute-start
  52.8 29.7 %all_gather.7 = bf16[768,4,2,64]{3,1,2,0:T(4,128)(2,1)S(1)} all-gather(bf16[192,4,2,64]{3,1,2,0:T(4,128)(2,1)S(1)} %copy.51), channel_id=1, replica_groups=mesh['ch'=4,'sx'=4,'sy'=2] {'ch'}, dimensions={0}, use_global_device_ids=true | all-gather | bytes 983040 | tf_op jit(solution)/shard_map/all_gather | solution.py:58
  83.5 3.2 collective-permute-start.8
  90.3 3.4 collective-permute-start.14
  96.3 4.6 collective-permute-start.2
  103.5 5.4 collective-permute-start.10
  164.4 5.0 fusion.255
  177.9 3.7 collective-permute-start.4
  182.9 2.5 fusion.112
  185.4 2.6 select_maximum_fusion
  188.1 6.0 fusion.254
  202.4 5.1 collective-permute-start.6
  212.2 2.8 collective-permute-done.7
  251.6 13.7 %bitcast_add_fusion = f32[768,512]{0,1:T(8,128)S(1)} fusion(f32[512,768]{1,0:T(8,128)} %fusion.87, f32[512,768]{1,0:T(8,128)} %fusion.90, f32[512,768]{1,0:T(8,128)} %fusion.92, f32[512,768]{1,0:T(8,128)} %fusion.94, f32[512,768]{1,0:T(8,128)} %fusion.96, f32[512,768]{1,0:T(8,128)} %fusion.98, f32[512,768]{1,0:T(8,128)} %fusion.100, ...), kind=kOutput, calls=%fused_computation.23 | convolution fusion | flops 161218560 | bytes 43024384 | tf_op jit(solution)/shard_map/dot_general | solution.py:49
  267.2 2.4 fusion.45
  269.7 2.3 fusion.44
  275.5 2.3 fusion.41
  285.9 21.4 %reduce-scatter.4.cloned.1.call-done = f32[192,512]{1,0:T(8,128)} async-done(((f32[768,512]{1,0:T(8,128)}), f32[192,512]{1,0:T(8,128)}) %reduce-scatter.4.cloned.1.call-update) | async-done | bytes 393232
  309.2 361.9 %all-reduce.7.cloned.1.call-done = (f32[27,192,768]{2,1,0:T(8,128)}, f32[27,192,768]{2,1,0:T(8,128)}) async-done(((f32[27,192,768]{2,1,0:T(8,128)}, f32[27,192,768]{2,1,0:T(8,128)}), (f32[27,192,768]{2,1,0:T(8,128)}, f32[27,192,768]{2,1,0:T(8,128)})) %all-reduce.7.cloned.1.call-update) | async-done | bytes 31850512 | tf_op jit(solution)/shard_map/psum | solution.py:90
  671.0 12.1 %broadcast_multiply_fusion.1 = f32[27,192,768]{2,1,0:T(8,128)} fusion(f32[27,192,768]{2,1,0:T(8,128)} %get-tuple-element.3), kind=kLoop, calls=%fused_computation.3 | loop fusion | flops 3981312 | bytes 31850496 | tf_op jit(solution)/shard_map/mul | solution.py:92
  683.2 3.8 copy-done.1
  686.9 6.1 broadcast_multiply_fusion
  (215 shorter events, 146.8 us)
Async XLA Ops:
  8.0 44.6 %copy-start.19 = (bf16[192,4,2,64]{0,3,2,1:T(8,128)(2,1)S(1)}, bf16[192,4,2,64]{0,3,2,1:T(8,128)(2,1)}, u32[]{:S(2)}) copy-start(bf16[192,4,2,64]{0,3,2,1:T(8,128)(2,1)} %param.5) | copy-start | bytes 589828
  8.0 299.3 %reduce-scatter.4.cloned.1.call-start = ((), (), s32[]{:S(2)}) async-start(), calls=%async_computation.1 | async-start | bytes 1966080
  9.7 78.2 %collective-permute-start.12 = (bf16[192,1,2,64]{0,3,2,1:T(8,128)(2,1)}, bf16[192,1,2,64]{0,3,2,1:T(8,128)(2,1)}, u32[]{:S(2)}, u32[]{:S(2)}) collective-permute-start(bf16[192,1,2,64]{0,3,2,1:T(8,128)(2,1)} %get-tuple-element.99), channel_id=1, source_target_pairs={{0,2},{2,4},{4,6},{1,3},{3,5},{5,7},{8,10},{10,12},{12,14},{9,11},... | collective-permute-start | bytes 147464 | tf_op jit(solution)/shard_map/ppermute | solution.py:16
  12.7 76.5 %collective-permute-start.13 = (bf16[192,1,2,64]{0,3,2,1:T(8,128)(2,1)}, bf16[192,1,2,64]{0,3,2,1:T(8,128)(2,1)}, u32[]{:S(2)}, u32[]{:S(2)}) collective-permute-start(bf16[192,1,2,64]{0,3,2,1:T(8,128)(2,1)} %get-tuple-element.100), channel_id=1, source_target_pairs={{2,0},{4,2},{6,4},{3,1},{5,3},{7,5},{10,8},{12,10},{14,12},{11,9},... | collective-permute-start | bytes 147464 | tf_op jit(solution)/shard_map/ppermute | solution.py:18
  47.6 46.1 %collective-permute-start = (bf16[768,1,2,64]{0,3,2,1:T(8,128)(2,1)}, bf16[768,1,2,64]{0,3,2,1:T(8,128)(2,1)}, u32[]{:S(2)}, u32[]{:S(2)}) collective-permute-start(bf16[768,1,2,64]{0,3,2,1:T(8,128)(2,1)} %get-tuple-element.85), channel_id=1, source_target_pairs={{0,2},{2,4},{4,6},{1,3},{3,5},{5,7},{8,10},{10,12},{12,14},{9,11},... | collective-permute-start | bytes 589832 | tf_op jit(solution)/shard_map/ppermute | solution.py:16
  51.3 43.7 %collective-permute-start.1 = (bf16[768,1,2,64]{0,3,2,1:T(8,128)(2,1)}, bf16[768,1,2,64]{0,3,2,1:T(8,128)(2,1)}, u32[]{:S(2)}, u32[]{:S(2)}) collective-permute-start(bf16[768,1,2,64]{0,3,2,1:T(8,128)(2,1)} %get-tuple-element.86), channel_id=1, source_target_pairs={{2,0},{4,2},{6,4},{3,1},{5,3},{7,5},{10,8},{12,10},{14,12},{11,9},... | collective-permute-start | bytes 589832 | tf_op jit(solution)/shard_map/ppermute | solution.py:18
  83.5 17.3 %collective-permute-start.8 = (bf16[768,1,2,64]{0,3,2,1:T(8,128)(2,1)S(1)}, bf16[768,1,2,64]{0,3,2,1:T(8,128)(2,1)S(1)}, u32[]{:S(2)}, u32[]{:S(2)}) collective-permute-start(bf16[768,1,2,64]{0,3,2,1:T(8,128)(2,1)S(1)} %get-tuple-element.81), channel_id=1, source_target_pairs={{0,2},{2,4},{4,6},{1,3},{3,5},{5,7},{8,10},{10,12},{12,14},{9,11},... | collective-permute-start | bytes 589832 | tf_op jit(solution)/shard_map/ppermute | solution.py:16
  88.0 14.2 %collective-permute-start.9 = (bf16[768,1,2,64]{0,3,2,1:T(8,128)(2,1)S(1)}, bf16[768,1,2,64]{0,3,2,1:T(8,128)(2,1)S(1)}, u32[]{:S(2)}, u32[]{:S(2)}) collective-permute-start(bf16[768,1,2,64]{0,3,2,1:T(8,128)(2,1)S(1)} %get-tuple-element.82), channel_id=1, source_target_pairs={{2,0},{4,2},{6,4},{3,1},{5,3},{7,5},{10,8},{12,10},{14,12},{11,9},... | collective-permute-start | bytes 589832 | tf_op jit(solution)/shard_map/ppermute | solution.py:18
  90.3 18.6 %collective-permute-start.14 = (bf16[192,6,1,64]{0,3,2,1:T(8,128)(2,1)S(1)}, bf16[192,6,1,64]{0,3,2,1:T(8,128)(2,1)S(1)}, u32[]{:S(2)}, u32[]{:S(2)}) collective-permute-start(bf16[192,6,1,64]{0,3,2,1:T(8,128)(2,1)S(1)} %get-tuple-element.93), channel_id=1, source_target_pairs={{0,1},{2,3},{4,5},{6,7},{8,9},{10,11},{12,13},{14,15},{16,17},{18,... | collective-permute-start | bytes 442376 | tf_op jit(solution)/shard_map/ppermute | solution.py:16
  93.7 16.8 %collective-permute-start.15 = (bf16[192,6,1,64]{0,3,2,1:T(8,128)(2,1)S(1)}, bf16[192,6,1,64]{0,3,2,1:T(8,128)(2,1)S(1)}, u32[]{:S(2)}, u32[]{:S(2)}) collective-permute-start(bf16[192,6,1,64]{0,3,2,1:T(8,128)(2,1)S(1)} %get-tuple-element.94), channel_id=1, source_target_pairs={{1,0},{3,2},{5,4},{7,6},{9,8},{11,10},{13,12},{15,14},{17,16},{19,... | collective-permute-start | bytes 442376 | tf_op jit(solution)/shard_map/ppermute | solution.py:18
  96.3 56.1 %collective-permute-start.2 = (bf16[768,6,1,64]{0,3,2,1:T(8,128)(2,1)S(1)}, bf16[768,6,1,64]{0,3,2,1:T(8,128)(2,1)S(1)}, u32[]{:S(2)}, u32[]{:S(2)}) collective-permute-start(bf16[768,6,1,64]{0,3,2,1:T(8,128)(2,1)S(1)} %get-tuple-element.59), channel_id=1, source_target_pairs={{0,1},{2,3},{4,5},{6,7},{8,9},{10,11},{12,13},{14,15},{16,17},{18,... | collective-permute-start | bytes 1769480 | tf_op jit(solution)/shard_map/ppermute | solution.py:16
  100.9 51.5 %collective-permute-start.3 = (bf16[768,6,1,64]{0,3,2,1:T(8,128)(2,1)S(1)}, bf16[768,6,1,64]{0,3,2,1:T(8,128)(2,1)S(1)}, u32[]{:S(2)}, u32[]{:S(2)}) collective-permute-start(bf16[768,6,1,64]{0,3,2,1:T(8,128)(2,1)S(1)} %get-tuple-element.60), channel_id=1, source_target_pairs={{1,0},{3,2},{5,4},{7,6},{9,8},{11,10},{13,12},{15,14},{17,16},{19,... | collective-permute-start | bytes 1769480 | tf_op jit(solution)/shard_map/ppermute | solution.py:18
  103.5 82.0 %collective-permute-start.10 = (bf16[768,6,1,64]{0,3,2,1:T(8,128)(2,1)}, bf16[768,6,1,64]{0,3,2,1:T(8,128)(2,1)}, u32[]{:S(2)}, u32[]{:S(2)}) collective-permute-start(bf16[768,6,1,64]{0,3,2,1:T(8,128)(2,1)} %get-tuple-element.55), channel_id=1, source_target_pairs={{0,1},{2,3},{4,5},{6,7},{8,9},{10,11},{12,13},{14,15},{16,17},{18,... | collective-permute-start | bytes 1769480 | tf_op jit(solution)/shard_map/ppermute | solution.py:16
  108.9 76.5 %collective-permute-start.11 = (bf16[768,6,1,64]{0,3,2,1:T(8,128)(2,1)}, bf16[768,6,1,64]{0,3,2,1:T(8,128)(2,1)}, u32[]{:S(2)}, u32[]{:S(2)}) collective-permute-start(bf16[768,6,1,64]{0,3,2,1:T(8,128)(2,1)} %get-tuple-element.56), channel_id=1, source_target_pairs={{1,0},{3,2},{5,4},{7,6},{9,8},{11,10},{13,12},{15,14},{17,16},{19,... | collective-permute-start | bytes 1769480 | tf_op jit(solution)/shard_map/ppermute | solution.py:18
  177.9 24.4 %collective-permute-start.4 = (bf16[192,1,2,64]{0,3,2,1:T(8,128)(2,1)S(1)}, bf16[192,1,2,64]{0,3,2,1:T(8,128)(2,1)S(1)}, u32[]{:S(2)}, u32[]{:S(2)}) collective-permute-start(bf16[192,1,2,64]{0,3,2,1:T(8,128)(2,1)S(1)} %get-tuple-element.103), channel_id=1, source_target_pairs={{0,2},{2,4},{4,6},{1,3},{3,5},{5,7},{8,10},{10,12},{12,14},{9,11},... | collective-permute-start | bytes 147464 | tf_op jit(solution)/shard_map/ppermute | solution.py:16
  181.6 20.7 %collective-permute-start.5 = (bf16[192,1,2,64]{0,3,2,1:T(8,128)(2,1)S(1)}, bf16[192,1,2,64]{0,3,2,1:T(8,128)(2,1)S(1)}, u32[]{:S(2)}, u32[]{:S(2)}) collective-permute-start(bf16[192,1,2,64]{0,3,2,1:T(8,128)(2,1)S(1)} %get-tuple-element.104), channel_id=1, source_target_pairs={{2,0},{4,2},{6,4},{3,1},{5,3},{7,5},{10,8},{12,10},{14,12},{11,9},... | collective-permute-start | bytes 147464 | tf_op jit(solution)/shard_map/ppermute | solution.py:18
  202.2 19.4 %copy-start = (f32[27,192,768]{2,1,0:T(8,128)}, f32[27,192,768]{2,1,0:T(8,128)S(1)}, u32[]{:S(2)}) copy-start(f32[27,192,768]{2,1,0:T(8,128)S(1)} %fusion.46) | copy-start | bytes 47775748
  202.4 9.8 %collective-permute-start.6 = (bf16[192,6,1,64]{0,3,2,1:T(8,128)(2,1)S(1)}, bf16[192,6,1,64]{0,3,2,1:T(8,128)(2,1)S(1)}, u32[]{:S(2)}, u32[]{:S(2)}) collective-permute-start(bf16[192,6,1,64]{0,3,2,1:T(8,128)(2,1)S(1)} %get-tuple-element.97), channel_id=1, source_target_pairs={{0,1},{2,3},{4,5},{6,7},{8,9},{10,11},{12,13},{14,15},{16,17},{18,... | collective-permute-start | bytes 442376 | tf_op jit(solution)/shard_map/ppermute | solution.py:16
  207.5 7.6 %collective-permute-start.7 = (bf16[192,6,1,64]{0,3,2,1:T(8,128)(2,1)S(1)}, bf16[192,6,1,64]{0,3,2,1:T(8,128)(2,1)S(1)}, u32[]{:S(2)}, u32[]{:S(2)}) collective-permute-start(bf16[192,6,1,64]{0,3,2,1:T(8,128)(2,1)S(1)} %get-tuple-element.98), channel_id=1, source_target_pairs={{1,0},{3,2},{5,4},{7,6},{9,8},{11,10},{13,12},{15,14},{17,16},{19,... | collective-permute-start | bytes 442376 | tf_op jit(solution)/shard_map/ppermute | solution.py:18
  266.9 12.1 %copy-start.5 = (bf16[768,4,2,64]{0,3,2,1:T(8,128)(2,1)S(1)}, bf16[768,4,2,64]{0,3,2,1:T(8,128)(2,1)}, u32[]{:S(2)}) copy-start(bf16[768,4,2,64]{0,3,2,1:T(8,128)(2,1)} %get-tuple-element.8) | copy-start | bytes 2359300
  266.9 404.1 %all-reduce.7.cloned.1.call-start = ((), (), s32[]{:S(2)}) async-start(), calls=%async_computation.2 | async-start | bytes 63700992 | tf_op jit(solution)/shard_map/psum | solution.py:90
  267.2 12.9 %copy-start.9 = (bf16[768,4,2,64]{0,3,2,1:T(8,128)(2,1)S(1)}, bf16[768,4,2,64]{0,3,2,1:T(8,128)(2,1)}, u32[]{:S(2)}) copy-start(bf16[768,4,2,64]{0,3,2,1:T(8,128)(2,1)} %get-tuple-element.79) | copy-start | bytes 2359300
  269.7 11.6 %copy-start.4 = (bf16[768,4,2,64]{0,3,2,1:T(8,128)(2,1)S(1)}, bf16[768,4,2,64]{0,3,2,1:T(8,128)(2,1)}, u32[]{:S(2)}) copy-start(bf16[768,4,2,64]{0,3,2,1:T(8,128)(2,1)} %get-tuple-element.7) | copy-start | bytes 2359300
  671.0 15.9 %copy-start.1 = (f32[27,192,768]{2,1,0:T(8,128)S(1)}, f32[27,192,768]{2,1,0:T(8,128)}, u32[]{:S(2)}) copy-start(f32[27,192,768]{2,1,0:T(8,128)} %get-tuple-element.4) | copy-start | bytes 47775748
  (18 other events, 108.1 us)
Sparse Core Ops, SparseCore 0:
  267.1 40.2 reduce-scatter.3
Sparse Core Ops, SparseCore 1:
  286.0 385.0 all-reduce.6
where the time goes:
time: 705 us; the launch traced here: 701 us
  waiting for transfers between devices  386 us (55%)
  matrix products  131 us (19%)
  blocking collectives  60.2 us (9%)
  starting transfers between devices  43.2 us (6%)
  other arithmetic  35.7 us (5%)
  local copies, waits for them, and re-layouts  27.8 us (4%)
  between operations  16.6 us (2%)
    psum x1, waiting for transfers between devices, shards(): filter_one, filter_two = lax.psum((filter_one, filter_two), ('sx', 'sy'))  362 us
    dot_general x54, matrix products, contract_positions(): lax.dot_general(left, right, (((1,), (1,)), ((), ())), preferred_element_...  60 us
    dot_general x27, matrix products, contract_first(): lax.dot_general(left, right, (((0,), (0,)), ((), ())), preferred_element_...  54.4 us
    ppermute x8, starting transfers between devices, padded_2(): lax.ppermute(tail, axis, [(i, (i + 1) % count) for i in range(ends)])  32.1 us
    all_gather x1, blocking collectives, shards(): lax.all_gather(out_grad, 'ch', axis=0, tiled=True)  30.6 us
    all_gather x1, blocking collectives, shards(): lax.all_gather(inputs, 'ch', axis=0, tiled=True)  29.7 us
    unnamed x3, waiting for transfers between devices  21.5 us
    mul x2, other arithmetic, shards(): return (input_grad, filter_one * factor, filter_two * factor)  18.3 us
  transfers between devices with their start and end apart: 18, of which 3 were waited for; matrix products, arithmetic and copies ran while one was open for 17% of the time, Pallas kernels for 0%

commit v1 on v0

--- a/solution.py
+++ b/solution.py
@@ -87,7 +87,7 @@
     input_grad = lax.psum_scatter(partial_terms, "ch", scatter_dimension=0, tiled=True).astype(
         jnp.bfloat16
     )
-    filter_one, filter_two = lax.psum((filter_one, filter_two), ("sx", "sy"))
+    filter_one, filter_two = lax.psum(lax.psum((filter_one, filter_two), "sy"), "sx")
     factor = 1.0 / math.sqrt(positions * lax.axis_size("sx") * lax.axis_size("sy"))
     return (input_grad, filter_one * factor, filter_two * factor)
 

time: 705 us -> 1510 us (2.14)
  waiting for transfers between devices: 386 us -> 1180 us
  matrix products: 131 us -> 148 us
    psum x1 -> x2, waiting for transfers between devices: 362 us -> 1160 us  [the longest x1 632 us: shards(): lax.psum((filter_one, filter_two), 'sy')]
    unnamed x3 -> x4, waiting for transfers between devices: 21.5 us -> 0.07 us
    dot_general x27, matrix products: 16.6 us -> 32.2 us  [shards(): jnp.dot(weight_two[offset], window(grad_pad, offset, True), preferred_ele...]
  transfers between devices with their start and end apart: 18 -> 19, of which waited for: 3 -> 5; matrix products, arithmetic and copies ran while one was open for 17% -> 9% of each run, Pallas kernels for 0% -> 0%
where the time goes in v1:
time: 1510 us; the launch traced here: 1500 us
  waiting for transfers between devices  1180 us (78%)
  matrix products  148 us (10%)
  blocking collectives  59.8 us (4%)
  starting transfers between devices  43.1 us (3%)
  other arithmetic  33.9 us (2%)
  local copies, waits for them, and re-layouts  27.1 us (2%)
  between operations  16.5 us (1%)
    psum x1, waiting for transfers between devices, shards(): lax.psum((filter_one, filter_two), 'sy')  632 us
    psum x1, waiting for transfers between devices, shards(): lax.psum(lax.psum((filter_one, filter_two), 'sy'), 'sx')  532 us
    dot_general x54, matrix products, contract_positions(): lax.dot_general(left, right, (((1,), (1,)), ((), ())), preferred_element_...  62.3 us
    dot_general x27, matrix products, contract_first(): lax.dot_general(left, right, (((0,), (0,)), ((), ())), preferred_element_...  53.9 us
    dot_general x27, matrix products, shards(): jnp.dot(weight_two[offset], window(grad_pad, offset, True), preferred_ele...  32.2 us
    ppermute x8, starting transfers between devices, padded_2(): lax.ppermute(tail, axis, [(i, (i + 1) % count) for i in range(ends)])  32.1 us
  transfers between devices with their start and end apart: 19, of which 5 were waited for; matrix products, arithmetic and copies ran while one was open for 9% of the time, Pallas kernels for 0%

profile of v1, /device:TPU:0, one launch (start us, length us, event | category | flops | bytes accessed | tf_op | source)
XLA Modules:
  0.0 1504.0 jit_solution(9270476792069884311)
XLA Ops:
  9.7 2.4 collective-permute-start.12
  14.6 30.0 %all_gather.6 = bf16[768,4,2,64]{3,1,2,0:T(4,128)(2,1)S(1)} all-gather(bf16[192,4,2,64]{3,1,2,0:T(4,128)(2,1)S(1)} %copy.42), channel_id=1, replica_groups=mesh['ch'=4,'sx'=4,'sy'=2] {'ch'}, dimensions={0}, use_global_device_ids=true | all-gather | bytes 983040 | tf_op jit(solution)/shard_map/all_gather | solution.py:59
  46.4 4.3 collective-permute-start
  52.2 29.8 %all_gather.7 = bf16[768,4,2,64]{3,1,2,0:T(4,128)(2,1)S(1)} all-gather(bf16[192,4,2,64]{3,1,2,0:T(4,128)(2,1)S(1)} %copy.51), channel_id=1, replica_groups=mesh['ch'=4,'sx'=4,'sy'=2] {'ch'}, dimensions={0}, use_global_device_ids=true | all-gather | bytes 983040 | tf_op jit(solution)/shard_map/all_gather | solution.py:58
  83.1 3.1 collective-permute-start.8
  88.9 3.4 collective-permute-start.14
  95.0 4.6 collective-permute-start.2
  102.1 5.4 collective-permute-start.10
  157.2 5.0 fusion.255
  182.1 2.5 select_maximum_fusion
  184.6 5.8 fusion.254
  193.5 2.9 convolution_add_fusion
  228.3 3.5 collective-permute-start.4
  234.6 2.9 collective-permute-done.5
  237.7 5.4 collective-permute-start.6
  246.0 2.6 fusion.130
  248.6 3.3 collective-permute-done.6
  251.9 4.5 collective-permute-done.7
  292.9 13.4 bitcast_add_fusion
  307.9 632.3 %all-reduce.11.cloned.1.call-done = (f32[27,192,768]{2,1,0:T(8,128)}, f32[27,192,768]{2,1,0:T(8,128)}) async-done(((f32[27,192,768]{2,1,0:T(8,128)}, f32[27,192,768]{2,1,0:T(8,128)}), (f32[27,192,768]{2,1,0:T(8,128)}, f32[27,192,768]{2,1,0:T(8,128)})) %all-reduce.11.cloned.1.call-update) | async-done | bytes 31850512 | tf_op jit(solution)/shard_map/psum | solution.py:90
  942.1 532.2 %all-reduce.9.cloned.1.call-done = (f32[27,192,768]{2,1,0:T(8,128)}, f32[27,192,768]{2,1,0:T(8,128)}) async-done(((f32[27,192,768]{2,1,0:T(8,128)}, f32[27,192,768]{2,1,0:T(8,128)}), (f32[27,192,768]{2,1,0:T(8,128)}, f32[27,192,768]{2,1,0:T(8,128)})) %all-reduce.9.cloned.1.call-update) | async-done | bytes 31850512 | tf_op jit(solution)/shard_map/psum | solution.py:90
  1474.3 12.1 broadcast_multiply_fusion.1
  1486.4 3.8 copy-done
  1490.2 6.1 broadcast_multiply_fusion
  (220 shorter events, 166.1 us)
Async XLA Ops:
  8.0 44.0 %copy-start.20 = (bf16[192,4,2,64]{0,3,2,1:T(8,128)(2,1)S(1)}, bf16[192,4,2,64]{0,3,2,1:T(8,128)(2,1)}, u32[]{:S(2)}) copy-start(bf16[192,4,2,64]{0,3,2,1:T(8,128)(2,1)} %param.5) | copy-start | bytes 589828
  8.0 932.2 %all-reduce.11.cloned.1.call-start = ((), (), s32[]{:S(2)}) async-start(), calls=%async_computation.3 | async-start | bytes 63700992 | tf_op jit(solution)/shard_map/psum | solution.py:90
  9.7 77.8 %collective-permute-start.12 = (bf16[192,1,2,64]{0,3,2,1:T(8,128)(2,1)}, bf16[192,1,2,64]{0,3,2,1:T(8,128)(2,1)S(1)}, u32[]{:S(2)}, u32[]{:S(2)}) collective-permute-start(bf16[192,1,2,64]{0,3,2,1:T(8,128)(2,1)} %get-tuple-element.101), channel_id=1, source_target_pairs={{0,2},{2,4},{4,6},{1,3},{3,5},{5,7},{8,10},{10,12},{12,14},{9,11},... | collective-permute-start | bytes 147464 | tf_op jit(solution)/shard_map/ppermute | solution.py:16
  12.1 76.7 %collective-permute-start.13 = (bf16[192,1,2,64]{0,3,2,1:T(8,128)(2,1)}, bf16[192,1,2,64]{0,3,2,1:T(8,128)(2,1)S(1)}, u32[]{:S(2)}, u32[]{:S(2)}) collective-permute-start(bf16[192,1,2,64]{0,3,2,1:T(8,128)(2,1)} %get-tuple-element.102), channel_id=1, source_target_pairs={{2,0},{4,2},{6,4},{3,1},{5,3},{7,5},{10,8},{12,10},{14,12},{11,9},... | collective-permute-start | bytes 147464 | tf_op jit(solution)/shard_map/ppermute | solution.py:18
  46.4 46.0 %collective-permute-start = (bf16[768,1,2,64]{0,3,2,1:T(8,128)(2,1)}, bf16[768,1,2,64]{0,3,2,1:T(8,128)(2,1)}, u32[]{:S(2)}, u32[]{:S(2)}) collective-permute-start(bf16[768,1,2,64]{0,3,2,1:T(8,128)(2,1)} %get-tuple-element.87), channel_id=1, source_target_pairs={{0,2},{2,4},{4,6},{1,3},{3,5},{5,7},{8,10},{10,12},{12,14},{9,11},... | collective-permute-start | bytes 589832 | tf_op jit(solution)/shard_map/ppermute | solution.py:16
  50.7 43.0 %collective-permute-start.1 = (bf16[768,1,2,64]{0,3,2,1:T(8,128)(2,1)}, bf16[768,1,2,64]{0,3,2,1:T(8,128)(2,1)}, u32[]{:S(2)}, u32[]{:S(2)}) collective-permute-start(bf16[768,1,2,64]{0,3,2,1:T(8,128)(2,1)} %get-tuple-element.88), channel_id=1, source_target_pairs={{2,0},{4,2},{6,4},{3,1},{5,3},{7,5},{10,8},{12,10},{14,12},{11,9},... | collective-permute-start | bytes 589832 | tf_op jit(solution)/shard_map/ppermute | solution.py:18
  83.1 16.4 %collective-permute-start.8 = (bf16[768,1,2,64]{0,3,2,1:T(8,128)(2,1)S(1)}, bf16[768,1,2,64]{0,3,2,1:T(8,128)(2,1)S(1)}, u32[]{:S(2)}, u32[]{:S(2)}) collective-permute-start(bf16[768,1,2,64]{0,3,2,1:T(8,128)(2,1)S(1)} %get-tuple-element.83), channel_id=1, source_target_pairs={{0,2},{2,4},{4,6},{1,3},{3,5},{5,7},{8,10},{10,12},{12,14},{9,11},... | collective-permute-start | bytes 589832 | tf_op jit(solution)/shard_map/ppermute | solution.py:16
  87.5 13.4 collective-permute-start.9
  88.9 18.6 %collective-permute-start.14 = (bf16[192,6,1,64]{0,3,2,1:T(8,128)(2,1)S(1)}, bf16[192,6,1,64]{0,3,2,1:T(8,128)(2,1)S(1)}, u32[]{:S(2)}, u32[]{:S(2)}) collective-permute-start(bf16[192,6,1,64]{0,3,2,1:T(8,128)(2,1)S(1)} %get-tuple-element.95), channel_id=1, source_target_pairs={{0,1},{2,3},{4,5},{6,7},{8,9},{10,11},{12,13},{14,15},{16,17},{18,... | collective-permute-start | bytes 442376 | tf_op jit(solution)/shard_map/ppermute | solution.py:16
  92.4 16.7 %collective-permute-start.15 = (bf16[192,6,1,64]{0,3,2,1:T(8,128)(2,1)S(1)}, bf16[192,6,1,64]{0,3,2,1:T(8,128)(2,1)S(1)}, u32[]{:S(2)}, u32[]{:S(2)}) collective-permute-start(bf16[192,6,1,64]{0,3,2,1:T(8,128)(2,1)S(1)} %get-tuple-element.96), channel_id=1, source_target_pairs={{1,0},{3,2},{5,4},{7,6},{9,8},{11,10},{13,12},{15,14},{17,16},{19,... | collective-permute-start | bytes 442376 | tf_op jit(solution)/shard_map/ppermute | solution.py:18
  95.0 50.2 %collective-permute-start.2 = (bf16[768,6,1,64]{0,3,2,1:T(8,128)(2,1)S(1)}, bf16[768,6,1,64]{0,3,2,1:T(8,128)(2,1)S(1)}, u32[]{:S(2)}, u32[]{:S(2)}) collective-permute-start(bf16[768,6,1,64]{0,3,2,1:T(8,128)(2,1)S(1)} %get-tuple-element.61), channel_id=1, source_target_pairs={{0,1},{2,3},{4,5},{6,7},{8,9},{10,11},{12,13},{14,15},{16,17},{18,... | collective-permute-start | bytes 1769480 | tf_op jit(solution)/shard_map/ppermute | solution.py:16
  99.6 45.6 %collective-permute-start.3 = (bf16[768,6,1,64]{0,3,2,1:T(8,128)(2,1)S(1)}, bf16[768,6,1,64]{0,3,2,1:T(8,128)(2,1)S(1)}, u32[]{:S(2)}, u32[]{:S(2)}) collective-permute-start(bf16[768,6,1,64]{0,3,2,1:T(8,128)(2,1)S(1)} %get-tuple-element.62), channel_id=1, source_target_pairs={{1,0},{3,2},{5,4},{7,6},{9,8},{11,10},{13,12},{15,14},{17,16},{19,... | collective-permute-start | bytes 1769480 | tf_op jit(solution)/shard_map/ppermute | solution.py:18
  102.1 80.0 %collective-permute-start.10 = (bf16[768,6,1,64]{0,3,2,1:T(8,128)(2,1)}, bf16[768,6,1,64]{0,3,2,1:T(8,128)(2,1)}, u32[]{:S(2)}, u32[]{:S(2)}) collective-permute-start(bf16[768,6,1,64]{0,3,2,1:T(8,128)(2,1)} %get-tuple-element.57), channel_id=1, source_target_pairs={{0,1},{2,3},{4,5},{6,7},{8,9},{10,11},{12,13},{14,15},{16,17},{18,... | collective-permute-start | bytes 1769480 | tf_op jit(solution)/shard_map/ppermute | solution.py:16
  107.5 74.6 %collective-permute-start.11 = (bf16[768,6,1,64]{0,3,2,1:T(8,128)(2,1)}, bf16[768,6,1,64]{0,3,2,1:T(8,128)(2,1)}, u32[]{:S(2)}, u32[]{:S(2)}) collective-permute-start(bf16[768,6,1,64]{0,3,2,1:T(8,128)(2,1)} %get-tuple-element.58), channel_id=1, source_target_pairs={{1,0},{3,2},{5,4},{7,6},{9,8},{11,10},{13,12},{15,14},{17,16},{19,... | collective-permute-start | bytes 1769480 | tf_op jit(solution)/shard_map/ppermute | solution.py:18
  131.7 8.2 slice-start.2
  228.1 712.2 %reduce-scatter.4.cloned.1.call-start = ((), (), s32[]{:S(2)}) async-start(), calls=%async_computation.1 | async-start | bytes 1966080
  228.3 6.3 collective-permute-start.4
  231.8 5.8 collective-permute-start.5
  233.1 24.1 %slice-start = ((s8[7962624]{0:T(1024)(128)(4,1)}), s8[4194304]{0:T(1024)(128)(4,1)S(1)}, s32[]{:S(2)}) async-start(s8[7962624]{0:T(1024)(128)(4,1)} %bitcast.808), calls=%async_computation.4 | async-start | bytes 8388608
  237.7 14.2 collective-permute-start.6
  243.0 13.4 collective-permute-start.7
  246.0 11.2 slice-start.1
  307.9 1166.4 %all-reduce.9.cloned.1.call-start = ((), (), s32[]{:S(2)}) async-start(), calls=%async_computation.2 | async-start | bytes 63700992 | tf_op jit(solution)/shard_map/psum | solution.py:90
  1474.3 15.9 %copy-start = (f32[27,192,768]{2,1,0:T(8,128)S(1)}, f32[27,192,768]{2,1,0:T(8,128)}, u32[]{:S(2)}) copy-start(f32[27,192,768]{2,1,0:T(8,128)} %get-tuple-element.4) | copy-start | bytes 47775748
  (20 other events, 74.0 us)
Sparse Core Ops, SparseCore 0:
  228.2 711.9 all-reduce.10
  942.8 531.4 all-reduce.8
Sparse Core Ops, SparseCore 1:
  308.0 37.4 reduce-scatter.3
